TPU v7x, 32 devices: a whole 2x2x4 slice. The times are simulated.
32 devices in a mesh: kpt: 2 (over x), row: 8 (over z, y), col: 2 (over core).
Axes of the slice: x: 2, y: 2, z: 4, core: 2. Of those that a mesh axis runs over, the one named last changes fastest.
Arguments:
- wannier: float32 [64, 32, 1024], P('kpt', ('row', 'col')), parts along dimension 0, may hold values from -6 to 6
- pairs: int32 [384, 2], replicated, may hold values from 0 to 31, as said below
- gmap: int32 [8192], replicated, may hold values from 1 to 32767, as said below
- screened: bfloat16 [4, 2, 8192, 8192], P('kpt', None, 'row', 'col'), parts along dimension 0, may hold values from -0.046875 to 0.046875
Outputs:
- coulomb: float32 [2, 2, 768, 384], P(None, None, ('kpt', 'row', 'col')), parts along dimension 2
There are 2 independent parts, one for each index of `kpt`. A program takes and returns all parts, laid end to end along the dimension named above; an argument that names none is the same for every part. Nothing has to cross between parts.
Inputs may be any that keep to these rules, and one draw needn't show every extreme that they name: `gmap`: 8192 distinct flat cells of the grid; cell 0 is never among them. `pairs`: in each row the first Wannier function is no greater than the second; no two rows are equal.
All inputs are finite; a program needn't handle non-finite values.
Results may differ from a plain program's by a relative error of at most 0.0082.
Values may be sent and summed in bfloat16 or wider, within the bound.
No kernel may reach another device: no remote copies, remote signals or barrier semaphores. Data moves between devices by JAX's collectives and lax.ppermute only.
A program may use at most 128 MiB of HBM per device.

v0:
```python
import math
import jax
import jax.numpy as jnp
from jax import lax
from jax.sharding import PartitionSpec as P

NW = 32
GX = 32
NG = 8192
NP = 384


def line_tables(side_len):
    positions = jnp.arange(side_len, dtype=jnp.int32)
    phase_index = positions[:, None] * positions[None, :] % side_len
    angles = phase_index.astype(jnp.float32) * (2.0 * math.pi / side_len)
    return (jnp.cos(angles), jnp.sin(angles))


def plane_transform(density):
    cosine, sine_table = line_tables(GX)
    highest = lax.Precision.HIGHEST
    shaped = density.reshape(-1, GX, GX)
    real_z = jnp.einsum("nyz,kz->nyk", shaped, cosine, precision=highest)
    imag_z = -jnp.einsum("nyz,kz->nyk", shaped, sine_table, precision=highest)
    new_real = jnp.einsum("jy,nyk->njk", cosine, real_z, precision=highest) + jnp.einsum(
        "jy,nyk->njk", sine_table, imag_z, precision=highest
    )
    new_imag = jnp.einsum("jy,nyk->njk", cosine, imag_z, precision=highest) - jnp.einsum(
        "jy,nyk->njk", sine_table, real_z, precision=highest
    )
    return (new_real.reshape(density.shape), new_imag.reshape(density.shape))


def line_transform(real_part, imag_part):
    cosine, sine_table = line_tables(GX)
    highest = lax.Precision.HIGHEST
    new_real = jnp.einsum("kn,pny->pky", cosine, real_part, precision=highest) + jnp.einsum(
        "kn,pny->pky", sine_table, imag_part, precision=highest
    )
    new_imag = jnp.einsum("kn,pny->pky", cosine, imag_part, precision=highest) - jnp.einsum(
        "kn,pny->pky", sine_table, real_part, precision=highest
    )
    return (new_real, new_imag)


def right_columns(screened, segment):
    w_real = screened[:, 0]
    w_imag = screened[:, 1]
    real_real = jnp.einsum("fgh,bh->fgb", w_real, segment[0], preferred_element_type=jnp.float32)
    imag_imag = jnp.einsum("fgh,bh->fgb", w_imag, segment[1], preferred_element_type=jnp.float32)
    real_imag = jnp.einsum("fgh,bh->fgb", w_real, segment[1], preferred_element_type=jnp.float32)
    imag_real = jnp.einsum("fgh,bh->fgb", w_imag, segment[0], preferred_element_type=jnp.float32)
    return jnp.stack([real_real - imag_imag, real_imag + imag_real], axis=1)


def shards(wannier, pairs, gmap, screened):
    planes = wannier.shape[1]
    grid_cells = wannier.shape[2]
    members = jnp.arange(NW, dtype=jnp.int32)[None, :]
    pick_first = (pairs[:, 0:1] == members).astype(jnp.float32)
    pick_second = (pairs[:, 1:2] == members).astype(jnp.float32)
    flat_rows = wannier.reshape(NW, -1)
    highest = lax.Precision.HIGHEST
    density = jnp.dot(pick_first, flat_rows, precision=highest) * jnp.dot(
        pick_second, flat_rows, precision=highest
    )
    density = density.reshape(NP, planes, grid_cells)
    arrived = lax.all_to_all(density, ("row", "col"), split_axis=0, concat_axis=1, tiled=True)
    real_part, imag_part = plane_transform(arrived)
    real_part, imag_part = line_transform(real_part, imag_part)
    owned = real_part.shape[0]
    norm_factor = 1.0 / math.sqrt(GX * GX * GX)
    rho_real = jnp.take(real_part.reshape(owned, -1), gmap, axis=1) * norm_factor
    rho_imag = jnp.take(imag_part.reshape(owned, -1), gmap, axis=1) * norm_factor
    rho = jnp.stack([rho_real, rho_imag], axis=0).astype(jnp.bfloat16)
    row_span = screened.shape[2]
    halves = lax.all_to_all(rho, "col", split_axis=2, concat_axis=1, tiled=True)
    screened_rho = right_columns(screened, lax.all_gather(halves, "row", axis=1, tiled=True))
    blocks = lax.all_to_all(rho, "row", split_axis=2, concat_axis=1, tiled=True)
    blocks = blocks.reshape(2, lax.axis_size("row"), owned, row_span)
    left_panel = lax.all_gather(blocks, "col", axis=2, tiled=True).reshape(2, NP, row_span)
    left_wide = left_panel.astype(jnp.float32)
    u_real = jnp.einsum(
        "ag,fgb->fab", left_wide[0], screened_rho[:, 0], precision=highest
    ) + jnp.einsum("ag,fgb->fab", left_wide[1], screened_rho[:, 1], precision=highest)
    u_imag = jnp.einsum(
        "ag,fgb->fab", left_wide[0], screened_rho[:, 1], precision=highest
    ) - jnp.einsum("ag,fgb->fab", left_wide[1], screened_rho[:, 0], precision=highest)
    partial_terms = jnp.stack([u_real, u_imag], axis=1) / math.sqrt(NG)
    summed = lax.psum(partial_terms, ("row", "col"))
    share_rows = NP // lax.axis_size(("row", "col"))
    return lax.dynamic_slice_in_dim(
        summed, lax.axis_index(("row", "col")) * share_rows, share_rows, 2
    )


def solution(mesh):
    return jax.shard_map(
        shards,
        mesh=mesh,
        in_specs=(P("kpt", ("row", "col"), None), P(), P(), P("kpt", None, "row", "col")),
        out_specs=P(None, None, ("kpt", "row", "col"), None),
        check_vma=False,
    )
```

profile of v0, /device:TPU:0, one launch (start us, length us, event | category | flops | bytes accessed | tf_op | source)
XLA Modules:
  0.0 687.3 jit_solution(8600309741713015094)
XLA Ops:
  11.3 3.8 reshape.35
  15.1 7.5 %all-to-all-start = ((f32[384,2,1024]{2,1,0:T(2,128)}), f32[384,2,1024]{2,1,0:T(2,128)S(1)}, u32[]{:S(2)}, u32[]{:S(2)}) async-start(f32[384,2,1024]{2,1,0:T(2,128)} %reshape.35), calls=%async_computation | async-start | bytes 6291456 | tf_op jit(solution)/shard_map/all_to_all | solution.py:69
  22.7 59.1 %all-to-all-done = f32[384,2,1024]{2,1,0:T(2,128)S(1)} async-done(((f32[384,2,1024]{2,1,0:T(2,128)}), f32[384,2,1024]{2,1,0:T(2,128)S(1)}, u32[]{:S(2)}, u32[]{:S(2)}) %all-to-all-start) | async-done | bytes 3145760 | tf_op jit(solution)/shard_map/all_to_all | solution.py:69
  82.9 2.4 copy.71
  85.3 7.6 %reshape.36 = f32[768,32,32]{2,1,0:T(8,128)} reshape(f32[24,16,2,1024]{3,2,1,0:T(2,128)S(1)} %copy.71) | data formatting | bytes 6291456 | tf_op jit(solution)/shard_map/reshape | solution.py:23
  92.9 9.2 %copy.72 = f32[768,32,32]{0,2,1:T(8,128)S(1)} copy(f32[768,32,32]{2,1,0:T(8,128)} %reshape.36) | data formatting | bytes 6291456 | tf_op jit(solution)/shard_map/reshape | solution.py:23
  102.1 3.0 convolution_negate_fusion
  105.1 3.0 fusion.72
  108.1 4.9 fusion.22
  113.1 5.2 fusion.24
  118.2 6.7 add_bitcast_fusion.1
  125.0 5.5 subtract_bitcast_fusion.1
  130.5 10.6 %copy.79 = f32[768,32,32]{2,1,0:T(8,128)} copy(f32[768,32,32]{0,1,2:T(8,128)S(1)} %subtract_bitcast_fusion.1) | data formatting | bytes 6291456 | tf_op jit(solution)/shard_map/sub | solution.py:29
  141.1 9.4 %reshape.38 = f32[24,32,1024]{2,1,0:T(8,128)S(1)} reshape(f32[768,32,32]{2,1,0:T(8,128)} %copy.79) | data formatting | bytes 6291456 | tf_op jit(solution)/shard_map/reshape | solution.py:32
  150.4 5.5 fusion.66
  155.9 11.4 %copy.76 = f32[768,32,32]{2,1,0:T(8,128)} copy(f32[768,32,32]{0,1,2:T(8,128)} %add_bitcast_fusion.1) | data formatting | bytes 6291456 | tf_op jit(solution)/shard_map/add | solution.py:26
  167.3 10.7 %reshape.37 = f32[24,32,1024]{2,1,0:T(8,128)} reshape(f32[768,32,32]{2,1,0:T(8,128)} %copy.76) | data formatting | bytes 6291456 | tf_op jit(solution)/shard_map/reshape | solution.py:32
  178.0 5.9 fusion.69
  184.0 5.5 subtract_bitcast_fusion
  189.5 5.6 add_bitcast_fusion
  195.1 10.3 %copy.89 = f32[24,32,1024]{0,2,1:T(8,128)} copy(f32[24,32,1024]{2,1,0:T(8,128)} %add_bitcast_fusion) | data formatting | bytes 6291456 | tf_op jit(solution)/shard_map/reshape | solution.py:74
  205.4 8.6 %copy.90 = f32[24,32,1024]{0,2,1:T(8,128)} copy(f32[24,32,1024]{2,1,0:T(8,128)S(1)} %copy-done.2) | data formatting | bytes 6291456 | tf_op jit(solution)/shard_map/reshape | solution.py:75
  214.0 33.6 %gather_fusion = f32[8192,24]{1,0:T(8,128)} fusion(f32[24,32768]{0,1:T(8,128)} %bitcast.144, s32[8192]{0:T(1024)S(1)} %fusion.57), kind=kCustom, calls=%fused_computation.clone | custom fusion | bytes 1605632 | tf_op jit(solution)/shard_map/jit(_take)/gather | solution.py:74
  247.6 33.6 %gather_fusion.1 = f32[8192,24]{1,0:T(8,128)} fusion(f32[24,32768]{0,1:T(8,128)} %bitcast.143, s32[8192]{0:T(1024)S(1)} %fusion.57), kind=kCustom, calls=%fused_computation.1.clone | custom fusion | bytes 1605632 | tf_op jit(solution)/shard_map/jit(_take)/gather | solution.py:75
  281.3 7.2 %fusion.30 = (bf16[1,24,8192]{1,2,0:T(8,128)(2,1)S(1)}, bf16[1,24,8192]{1,2,0:T(8,128)(2,1)S(1)}) fusion(f32[8192,24]{1,0:T(8,128)} %gather_fusion, pred[8192]{0:T(1024)(128)(4,1)S(1)} %compare_and_fusion, f32[8192,24]{1,0:T(8,128)} %gather_fusion.1), kind=kLoop, calls=%fused_computation.43 | loop fusion | flops 1179648 | bytes 2367488 | tf_op jit(solution)/shard_map/stack | solution.py:76
  289.4 35.5 %copy.108 = bf16[2,24,8192]{1,0,2:T(2,128)(2,1)} copy(bf16[2,24,8192]{1,2,0:T(8,128)(2,1)S(1)} %pad_maximum_fusion) | data formatting | bytes 1572864 | tf_op jit(solution)/shard_map/stack | solution.py:76
  324.9 6.6 reshape.71
  331.5 35.8 %all_to_all.48 = bf16[8,2,24576]{2,1,0:T(2,128)(2,1)S(1)} all-to-all(bf16[8,2,24576]{2,1,0:T(2,128)(2,1)S(1)} %reshape.71), channel_id=1, replica_groups=mesh['kpt'=2,'row'=8,'col'=2] {'row'}, dimensions={0} | all-to-all | bytes 1572864 | tf_op jit(solution)/shard_map/all_to_all | solution.py:80
  367.3 6.9 %reshape.72 = bf16[8192,2,24]{2,1,0:T(2,128)(2,1)} reshape(bf16[8,2,24576]{2,1,0:T(2,128)(2,1)S(1)} %all_to_all.48) | data formatting | bytes 1572864
  374.3 10.3 %copy.87 = bf16[2,24,8,1024]{3,1,2,0:T(8,128)(2,1)} copy(bf16[2,24,8,1024]{1,0,3,2:T(2,128)(2,1)} %bitcast.145) | data formatting | bytes 1572864 | tf_op jit(solution)/shard_map/all_to_all | solution.py:80
  384.6 10.2 %copy.109 = bf16[2,24,8192]{1,0,2:T(2,128)(2,1)} copy(bf16[2,24,8192]{1,2,0:T(8,128)(2,1)} %copy-done) | data formatting | bytes 1572864 | tf_op jit(solution)/shard_map/stack | solution.py:76
  394.8 7.0 %reshape.73 = bf16[2,2,98304]{2,1,0:T(2,128)(2,1)S(1)} reshape(bf16[8192,2,24]{2,1,0:T(2,128)(2,1)} %bitcast.147) | data formatting | bytes 1572864
  401.9 4.4 all_to_all.49
  406.2 7.3 %reshape.74 = bf16[8192,2,24]{2,1,0:T(2,128)(2,1)} reshape(bf16[2,2,98304]{2,1,0:T(2,128)(2,1)S(1)} %all_to_all.49) | data formatting | bytes 1572864
  413.6 9.5 %copy.83 = bf16[2,24,2,4096]{3,1,2,0:T(8,128)(2,1)} copy(bf16[2,24,2,4096]{1,0,3,2:T(2,128)(2,1)} %bitcast.146) | data formatting | bytes 1572864 | tf_op jit(solution)/shard_map/all_to_all | solution.py:78
  423.1 1.5 fusion.129
  424.7 96.3 %all-gather.3.cloned.1.call-done = bf16[2,384,4096]{2,1,0:T(8,128)(2,1)} async-done(((bf16[2,48,4096]{2,1,0:T(8,128)(2,1)}), bf16[2,384,4096]{2,1,0:T(8,128)(2,1)}) %all-gather.3.cloned.1.call-update) | async-done | bytes 6291472 | tf_op jit(solution)/shard_map/all_gather | solution.py:79
  521.0 11.4 %fusion = f32[384,2,1024]{2,0,1:T(8,128)S(1)} fusion(bf16[2,2,1024,4096]{3,2,1,0:T(8,128)(2,1)} %param.9, bf16[2,384,4096]{2,1,0:T(8,128)(2,1)} %all-gather.3.cloned.1.call-done), kind=kOutput, calls=%fused_computation.2 | convolution fusion | flops 6442450944 | bytes 23068672 | tf_op jit(solution)/shard_map/fgh,bh->fgb/dot_general | solution.py:53
  532.4 11.2 %fusion.39 = f32[384,2,1024]{2,0,1:T(8,128)S(1)} fusion(f32[384,2,1024]{2,0,1:T(8,128)S(1)} %fusion, bf16[2,2,1024,4096]{3,2,1,0:T(8,128)(2,1)} %param.9, bf16[2,384,4096]{2,1,0:T(8,128)(2,1)} %all-gather.3.cloned.1.call-done), kind=kOutput, calls=%fused_computation.47 | convolution fusion | flops 6443237376 | bytes 26214400 | tf_op jit(solution)/shard_map/fgh,bh->fgb/dot_general | solution.py:52
  543.6 2.6 fusion.14
  546.2 2.6 fusion.16
  548.9 12.6 %fusion.2 = f32[384,2,1024]{2,0,1:T(8,128)} fusion(bf16[2,2,1024,4096]{3,2,1,0:T(8,128)(2,1)} %param.9, bf16[2,384,4096]{2,1,0:T(8,128)(2,1)} %all-gather.3.cloned.1.call-done), kind=kOutput, calls=%fused_computation.4 | convolution fusion | flops 6442450944 | bytes 23068672 | tf_op jit(solution)/shard_map/fgh,bh->fgb/dot_general | solution.py:51
  561.5 12.1 %fusion.36 = f32[384,2,1024]{2,0,1:T(8,128)S(1)} fusion(f32[384,2,1024]{2,0,1:T(8,128)} %fusion.2, bf16[2,2,1024,4096]{3,2,1,0:T(8,128)(2,1)} %param.9, bf16[2,384,4096]{2,1,0:T(8,128)(2,1)} %all-gather.3.cloned.1.call-done), kind=kOutput, calls=%fused_computation.46 | convolution fusion | flops 6443237376 | bytes 26214400 | tf_op jit(solution)/shard_map/fgh,bh->fgb/dot_general | solution.py:50
  573.6 2.7 fusion.48
  576.3 2.7 fusion.51
  579.0 1.6 maximum_multiply_fusion
  580.6 97.4 %all-reduce.2.cloned.1.call-done = f32[2,2,384,384]{2,3,0,1:T(8,128)} async-done(((f32[2,2,384,384]{2,3,0,1:T(8,128)}), f32[2,2,384,384]{2,3,0,1:T(8,128)}) %all-reduce.2.cloned.1.call-update) | async-done | bytes 2359312 | tf_op jit(solution)/shard_map/psum | solution.py:91
  678.0 1.7 constant_dynamic-slice_fusion
  (26 shorter events, 7.9 us)
Async XLA Ops:
  15.1 7.6 %copy-start.4 = (s32[8192]{0:T(1024)S(1)}, s32[8192]{0:T(1024)}, u32[]{:S(2)}) copy-start(s32[8192]{0:T(1024)} %param.8) | copy-start | bytes 98308
  15.1 66.8 %all-to-all-start = ((f32[384,2,1024]{2,1,0:T(2,128)}), f32[384,2,1024]{2,1,0:T(2,128)S(1)}, u32[]{:S(2)}, u32[]{:S(2)}) async-start(f32[384,2,1024]{2,1,0:T(2,128)} %reshape.35), calls=%async_computation | async-start | bytes 6291456 | tf_op jit(solution)/shard_map/all_to_all | solution.py:69
  22.6 400.5 %all-gather.5.cloned.1.call-start = ((), (), s32[]{:S(2)}) async-start(), calls=%async_computation.4 | async-start | bytes 2359296 | tf_op jit(solution)/shard_map/all_gather | solution.py:82
  178.0 6.0 copy-start.1
  178.0 6.0 copy-start.3
  195.1 10.3 %copy-start.2 = (f32[24,32,1024]{2,1,0:T(8,128)S(1)}, f32[24,32,1024]{2,1,0:T(8,128)}, u32[]{:S(2)}) copy-start(f32[24,32,1024]{2,1,0:T(8,128)} %subtract_bitcast_fusion) | copy-start | bytes 9437188
  289.4 35.5 %copy-start = (bf16[2,24,8192]{1,2,0:T(8,128)(2,1)}, bf16[2,24,8192]{1,2,0:T(8,128)(2,1)S(1)}, u32[]{:S(2)}) copy-start(bf16[2,24,8192]{1,2,0:T(8,128)(2,1)S(1)} %pad_maximum_fusion) | copy-start | bytes 2359300
  384.6 136.4 %all-gather.3.cloned.1.call-start = ((), (), s32[]{:S(2)}) async-start(), calls=%async_computation.3 | async-start | bytes 7077888 | tf_op jit(solution)/shard_map/all_gather | solution.py:79
  423.1 254.9 %all-reduce.2.cloned.1.call-start = ((), (), s32[]{:S(2)}) async-start(), calls=%async_computation.5 | async-start | bytes 4718592 | tf_op jit(solution)/shard_map/psum | solution.py:91
Sparse Core Ops, SparseCore 0:
  384.7 8.8 all-gather.4
  423.2 97.7 all-gather.2
  580.7 97.1 all-reduce.1
where the time goes:
time: 696 us; the launch traced here: 687 us
  waiting for transfers between devices  253 us (36%)
  local copies, waits for them, and re-layouts  251 us (36%)
  matrix products  112 us (16%)
  blocking collectives  40.2 us (6%)
  between operations  13.7 us (2%)
  other arithmetic  9.75 us (1%)
  starting transfers between devices  7.67 us (1%)
    psum x1, waiting for transfers between devices, shards(): summed = lax.psum(partial_terms, ('row', 'col'))  97.4 us
    all_gather x1, waiting for transfers between devices, shards(): lax.all_gather(halves, 'row', axis=1, tiled=True)  96.3 us
    all_to_all x1, waiting for transfers between devices, shards(): lax.all_to_all(density, ('row', 'col'), split_axis=0, concat_axis=1, tile...  59.1 us
    another operation x2, local copies, waits for them, and re-layouts, shards(): rho = jnp.stack([rho_real, rho_imag], axis=0).astype(jnp.bfloat16)  45.7 us
    all_to_all x1, blocking collectives, shards(): blocks = lax.all_to_all(rho, 'row', split_axis=2, concat_axis=1, tiled=True)  35.8 us
    gather x1, local copies, waits for them, and re-layouts, shards(): jnp.take(imag_part.reshape(owned, -1), gmap, axis=1) * norm_factor  33.6 us
    gather x1, local copies, waits for them, and re-layouts, shards(): jnp.take(real_part.reshape(owned, -1), gmap, axis=1) * norm_factor  33.6 us
    unnamed x15, local copies, waits for them, and re-layouts  29 us
  transfers between devices with their start and end apart: 4, of which 3 were waited for; matrix products, arithmetic and copies ran while one was open for 5% of the time, Pallas kernels for 0%

commit v1 on v0

--- a/solution.py
+++ b/solution.py
@@ -76,7 +76,7 @@
     rho = jnp.stack([rho_real, rho_imag], axis=0).astype(jnp.bfloat16)
     row_span = screened.shape[2]
     halves = lax.all_to_all(rho, "col", split_axis=2, concat_axis=1, tiled=True)
-    screened_rho = right_columns(screened, lax.all_gather(halves, "row", axis=1, tiled=True))
+    screened_rho = right_columns(screened, jnp.concatenate(lax.all_gather(halves, "row"), axis=1))
     blocks = lax.all_to_all(rho, "row", split_axis=2, concat_axis=1, tiled=True)
     blocks = blocks.reshape(2, lax.axis_size("row"), owned, row_span)
     left_panel = lax.all_gather(blocks, "col", axis=2, tiled=True).reshape(2, NP, row_span)

time: 696 us -> 697 us (level)
  no operation moved by 1% of the time
where the time goes in v1:
time: 697 us; the launch traced here: 688 us
  local copies, waits for them, and re-layouts  255 us (37%)
  waiting for transfers between devices  253 us (36%)
  matrix products  109 us (16%)
  blocking collectives  40.1 us (6%)
  between operations  13.6 us (2%)
  other arithmetic  9.52 us (1%)
  starting transfers between devices  7.67 us (1%)
    psum x1, waiting for transfers between devices, shards(): summed = lax.psum(partial_terms, ('row', 'col'))  97.4 us
    all_gather x1, waiting for transfers between devices, shards(): lax.all_gather(halves, 'row')  96.3 us
    all_to_all x1, waiting for transfers between devices, shards(): lax.all_to_all(density, ('row', 'col'), split_axis=0, concat_axis=1, tile...  59.1 us
    another operation x2, local copies, waits for them, and re-layouts, shards(): rho = jnp.stack([rho_real, rho_imag], axis=0).astype(jnp.bfloat16)  45.7 us
    all_to_all x1, blocking collectives, shards(): blocks = lax.all_to_all(rho, 'row', split_axis=2, concat_axis=1, tiled=True)  35.8 us
    gather x1, local copies, waits for them, and re-layouts, shards(): jnp.take(real_part.reshape(owned, -1), gmap, axis=1) * norm_factor  33.5 us
    gather x1, local copies, waits for them, and re-layouts, shards(): jnp.take(imag_part.reshape(owned, -1), gmap, axis=1) * norm_factor  33.5 us
    unnamed x15, local copies, waits for them, and re-layouts  29 us
  transfers between devices with their start and end apart: 4, of which 3 were waited for; matrix products, arithmetic and copies ran while one was open for 5% of the time, Pallas kernels for 0%

profile of v1, /device:TPU:0, one launch (start us, length us, event | category | flops | bytes accessed | tf_op | source)
XLA Modules:
  0.0 688.2 jit_solution(820082696855232240)
XLA Ops:
  11.3 3.8 reshape.44
  15.1 7.5 %all-to-all-start = ((f32[384,2,1024]{2,1,0:T(2,128)}), f32[384,2,1024]{2,1,0:T(2,128)S(1)}, u32[]{:S(2)}, u32[]{:S(2)}) async-start(f32[384,2,1024]{2,1,0:T(2,128)} %reshape.44), calls=%async_computation | async-start | bytes 6291456 | tf_op jit(solution)/shard_map/all_to_all | solution.py:69
  22.7 59.1 %all-to-all-done = f32[384,2,1024]{2,1,0:T(2,128)S(1)} async-done(((f32[384,2,1024]{2,1,0:T(2,128)}), f32[384,2,1024]{2,1,0:T(2,128)S(1)}, u32[]{:S(2)}, u32[]{:S(2)}) %all-to-all-start) | async-done | bytes 3145760 | tf_op jit(solution)/shard_map/all_to_all | solution.py:69
  82.9 2.4 copy.71
  85.3 7.5 %reshape.45 = f32[768,32,32]{2,1,0:T(8,128)} reshape(f32[24,16,2,1024]{3,2,1,0:T(2,128)S(1)} %copy.71) | data formatting | bytes 6291456 | tf_op jit(solution)/shard_map/reshape | solution.py:23
  92.8 9.5 %copy.72 = f32[768,32,32]{0,2,1:T(8,128)S(1)} copy(f32[768,32,32]{2,1,0:T(8,128)} %reshape.45) | data formatting | bytes 6291456 | tf_op jit(solution)/shard_map/reshape | solution.py:23
  102.3 3.0 convolution_negate_fusion
  105.4 3.0 fusion.72
  108.4 4.9 fusion.22
  113.3 5.1 fusion.24
  118.4 6.7 add_bitcast_fusion.1
  125.2 5.3 subtract_bitcast_fusion.1
  130.5 10.6 %copy.79 = f32[768,32,32]{2,1,0:T(8,128)} copy(f32[768,32,32]{0,1,2:T(8,128)S(1)} %subtract_bitcast_fusion.1) | data formatting | bytes 6291456 | tf_op jit(solution)/shard_map/sub | solution.py:29
  141.1 9.4 %reshape.47 = f32[24,32,1024]{2,1,0:T(8,128)S(1)} reshape(f32[768,32,32]{2,1,0:T(8,128)} %copy.79) | data formatting | bytes 6291456 | tf_op jit(solution)/shard_map/reshape | solution.py:32
  150.4 5.5 fusion.66
  155.9 11.4 %copy.76 = f32[768,32,32]{2,1,0:T(8,128)} copy(f32[768,32,32]{0,1,2:T(8,128)} %add_bitcast_fusion.1) | data formatting | bytes 6291456 | tf_op jit(solution)/shard_map/add | solution.py:26
  167.3 10.9 %reshape.46 = f32[24,32,1024]{2,1,0:T(8,128)} reshape(f32[768,32,32]{2,1,0:T(8,128)} %copy.76) | data formatting | bytes 6291456 | tf_op jit(solution)/shard_map/reshape | solution.py:32
  178.3 5.9 fusion.69
  184.3 5.5 subtract_bitcast_fusion
  189.8 5.6 add_bitcast_fusion
  195.4 10.2 %copy.89 = f32[24,32,1024]{0,2,1:T(8,128)} copy(f32[24,32,1024]{2,1,0:T(8,128)} %add_bitcast_fusion) | data formatting | bytes 6291456 | tf_op jit(solution)/shard_map/reshape | solution.py:74
  205.6 8.5 %copy.90 = f32[24,32,1024]{0,2,1:T(8,128)} copy(f32[24,32,1024]{2,1,0:T(8,128)S(1)} %copy-done.2) | data formatting | bytes 6291456 | tf_op jit(solution)/shard_map/reshape | solution.py:75
  214.2 33.5 %gather_fusion = f32[8192,24]{1,0:T(8,128)} fusion(f32[24,32768]{0,1:T(8,128)} %bitcast.141, s32[8192]{0:T(1024)S(1)} %fusion.57), kind=kCustom, calls=%fused_computation.clone | custom fusion | bytes 1605632 | tf_op jit(solution)/shard_map/jit(_take)/gather | solution.py:74
  247.7 33.5 %gather_fusion.1 = f32[8192,24]{1,0:T(8,128)} fusion(f32[24,32768]{0,1:T(8,128)} %bitcast.140, s32[8192]{0:T(1024)S(1)} %fusion.57), kind=kCustom, calls=%fused_computation.1.clone | custom fusion | bytes 1605632 | tf_op jit(solution)/shard_map/jit(_take)/gather | solution.py:75
  281.1 6.9 %fusion.30 = (bf16[1,24,8192]{1,2,0:T(8,128)(2,1)S(1)}, bf16[1,24,8192]{1,2,0:T(8,128)(2,1)S(1)}) fusion(f32[8192,24]{1,0:T(8,128)} %gather_fusion, pred[8192]{0:T(1024)(128)(4,1)S(1)} %compare_and_fusion, f32[8192,24]{1,0:T(8,128)} %gather_fusion.1), kind=kLoop, calls=%fused_computation.41 | loop fusion | flops 1179648 | bytes 2367488 | tf_op jit(solution)/shard_map/stack | solution.py:76
  289.0 35.5 %copy.108 = bf16[2,24,8192]{1,0,2:T(2,128)(2,1)} copy(bf16[2,24,8192]{1,2,0:T(8,128)(2,1)S(1)} %pad_maximum_fusion) | data formatting | bytes 1572864 | tf_op jit(solution)/shard_map/stack | solution.py:76
  324.5 6.6 reshape.81
  331.1 35.8 %all_to_all.45 = bf16[8,2,24576]{2,1,0:T(2,128)(2,1)S(1)} all-to-all(bf16[8,2,24576]{2,1,0:T(2,128)(2,1)S(1)} %reshape.81), channel_id=1, replica_groups=mesh['kpt'=2,'row'=8,'col'=2] {'row'}, dimensions={0} | all-to-all | bytes 1572864 | tf_op jit(solution)/shard_map/all_to_all | solution.py:80
  366.9 6.9 %reshape.82 = bf16[8192,2,24]{2,1,0:T(2,128)(2,1)} reshape(bf16[8,2,24576]{2,1,0:T(2,128)(2,1)S(1)} %all_to_all.45) | data formatting | bytes 1572864
  373.9 10.3 %copy.87 = bf16[2,24,8,1024]{3,1,2,0:T(8,128)(2,1)} copy(bf16[2,24,8,1024]{1,0,3,2:T(2,128)(2,1)} %bitcast.142) | data formatting | bytes 1572864 | tf_op jit(solution)/shard_map/all_to_all | solution.py:80
  384.2 10.2 %copy.109 = bf16[2,24,8192]{1,0,2:T(2,128)(2,1)} copy(bf16[2,24,8192]{1,2,0:T(8,128)(2,1)} %copy-done) | data formatting | bytes 1572864 | tf_op jit(solution)/shard_map/stack | solution.py:76
  394.4 7.0 %reshape.83 = bf16[2,2,98304]{2,1,0:T(2,128)(2,1)S(1)} reshape(bf16[8192,2,24]{2,1,0:T(2,128)(2,1)} %bitcast.144) | data formatting | bytes 1572864
  401.5 4.4 all_to_all.46
  405.8 7.3 %reshape.84 = bf16[8192,2,24]{2,1,0:T(2,128)(2,1)} reshape(bf16[2,2,98304]{2,1,0:T(2,128)(2,1)S(1)} %all_to_all.46) | data formatting | bytes 1572864
  413.1 9.4 %copy.83 = bf16[2,2,24,4096]{3,2,1,0:T(8,128)(2,1)} copy(bf16[2,2,24,4096]{2,0,3,1:T(2,128)(2,1)} %bitcast.143) | data formatting | bytes 1572864 | tf_op jit(solution)/shard_map/all_to_all | solution.py:78
  424.2 96.3 %all-gather.3.cloned.1.call-done = bf16[8,2,48,4096]{3,2,0,1:T(8,128)(2,1)} async-done(((bf16[1,2,48,4096]{3,2,0,1:T(8,128)(2,1)}), bf16[8,2,48,4096]{3,2,0,1:T(8,128)(2,1)}) %all-gather.3.cloned.1.call-update) | async-done | bytes 6291472 | tf_op jit(solution)/shard_map/all_gather | solution.py:79
  520.5 3.6 fusion.129
  524.2 11.9 %fusion = f32[384,2,1024]{2,0,1:T(8,128)} fusion(bf16[384,4096,1]{1,0,2:T(8,128)(2,1)S(1)} %bitcast.154, bf16[2,2,1024,4096]{3,2,1,0:T(8,128)(2,1)} %param.9), kind=kOutput, calls=%fused_computation.2 | convolution fusion | flops 6442450944 | bytes 23068672 | tf_op jit(solution)/shard_map/fgh,bh->fgb/dot_general | solution.py:53
  536.1 11.5 %fusion.2 = f32[384,2,1024]{2,0,1:T(8,128)} fusion(bf16[384,4096,1]{1,0,2:T(8,128)(2,1)S(1)} %bitcast.156, bf16[2,2,1024,4096]{3,2,1,0:T(8,128)(2,1)} %param.9), kind=kOutput, calls=%fused_computation.4 | convolution fusion | flops 6442450944 | bytes 23068672 | tf_op jit(solution)/shard_map/fgh,bh->fgb/dot_general | solution.py:51
  547.6 10.9 %fusion.39 = f32[384,2,1024]{2,0,1:T(8,128)S(1)} fusion(f32[384,2,1024]{2,0,1:T(8,128)} %fusion, bf16[384,4096,1]{1,0,2:T(8,128)(2,1)S(1)} %bitcast.157, bf16[2,2,1024,4096]{3,2,1,0:T(8,128)(2,1)} %param.9), kind=kOutput, calls=%fused_computation.45 | convolution fusion | flops 6443237376 | bytes 26214400 | tf_op jit(solution)/shard_map/fgh,bh->fgb/dot_general | solution.py:52
  558.4 10.9 %fusion.36 = f32[384,2,1024]{2,0,1:T(8,128)S(1)} fusion(f32[384,2,1024]{2,0,1:T(8,128)} %fusion.2, bf16[384,4096,1]{1,0,2:T(8,128)(2,1)S(1)} %bitcast.155, bf16[2,2,1024,4096]{3,2,1,0:T(8,128)(2,1)} %param.9), kind=kOutput, calls=%fused_computation.44 | convolution fusion | flops 6443237376 | bytes 26214400 | tf_op jit(solution)/shard_map/fgh,bh->fgb/dot_general | solution.py:50
  569.4 2.6 fusion.14
  572.0 2.6 fusion.16
  574.6 2.6 fusion.48
  577.2 2.6 fusion.51
  579.8 1.6 maximum_multiply_fusion
  581.4 97.4 %all-reduce.2.cloned.1.call-done = f32[2,2,384,384]{2,3,0,1:T(8,128)} async-done(((f32[2,2,384,384]{2,3,0,1:T(8,128)}), f32[2,2,384,384]{2,3,0,1:T(8,128)}) %all-reduce.2.cloned.1.call-update) | async-done | bytes 2359312 | tf_op jit(solution)/shard_map/psum | solution.py:91
  678.9 1.7 constant_dynamic-slice_fusion
  (27 shorter events, 9.4 us)
Async XLA Ops:
  15.1 7.6 %copy-start.4 = (s32[8192]{0:T(1024)S(1)}, s32[8192]{0:T(1024)}, u32[]{:S(2)}) copy-start(s32[8192]{0:T(1024)} %param.8) | copy-start | bytes 98308
  15.1 66.8 %all-to-all-start = ((f32[384,2,1024]{2,1,0:T(2,128)}), f32[384,2,1024]{2,1,0:T(2,128)S(1)}, u32[]{:S(2)}, u32[]{:S(2)}) async-start(f32[384,2,1024]{2,1,0:T(2,128)} %reshape.44), calls=%async_computation | async-start | bytes 6291456 | tf_op jit(solution)/shard_map/all_to_all | solution.py:69
  22.6 400.1 %all-gather.5.cloned.1.call-start = ((), (), s32[]{:S(2)}) async-start(), calls=%async_computation.4 | async-start | bytes 2359296 | tf_op jit(solution)/shard_map/all_gather | solution.py:82
  178.3 6.0 copy-start.1
  178.3 6.0 copy-start.3
  195.4 10.2 %copy-start.2 = (f32[24,32,1024]{2,1,0:T(8,128)S(1)}, f32[24,32,1024]{2,1,0:T(8,128)}, u32[]{:S(2)}) copy-start(f32[24,32,1024]{2,1,0:T(8,128)} %subtract_bitcast_fusion) | copy-start | bytes 9437188
  289.0 35.5 %copy-start = (bf16[2,24,8192]{1,2,0:T(8,128)(2,1)}, bf16[2,24,8192]{1,2,0:T(8,128)(2,1)S(1)}, u32[]{:S(2)}) copy-start(bf16[2,24,8192]{1,2,0:T(8,128)(2,1)S(1)} %pad_maximum_fusion) | copy-start | bytes 2359300
  384.2 136.3 %all-gather.3.cloned.1.call-start = ((), (), s32[]{:S(2)}) async-start(), calls=%async_computation.3 | async-start | bytes 7077888 | tf_op jit(solution)/shard_map/all_gather | solution.py:79
  422.6 256.3 %all-reduce.2.cloned.1.call-start = ((), (), s32[]{:S(2)}) async-start(), calls=%async_computation.5 | async-start | bytes 4718592 | tf_op jit(solution)/shard_map/psum | solution.py:91
Sparse Core Ops, SparseCore 0:
  384.3 8.8 all-gather.4
  422.7 97.7 all-gather.2
  581.5 97.2 all-reduce.1
